TPU v7x, 256 devices: a whole 4x4x8 slice. The times are simulated.
256 devices in a mesh: seq: 32 (over z, y), head: 8 (over x, core).
Axes of the slice: x: 4, y: 4, z: 8, core: 2. Of those that a mesh axis runs over, the one named last changes fastest.
Arguments:
- queries: bfloat16 [32768, 12288], P(('seq', 'head')), may hold values from -8 to 8
- latent: bfloat16 [32768, 512], P(('seq', 'head')), may hold values from -6 to 6
- rope_keys: bfloat16 [32768, 64], P(('seq', 'head')), may hold values from -8 to 8
- key_weight: bfloat16 [512, 8192], P('seq', 'head'), may hold values from -0.25 to 0.25
- value_weight: bfloat16 [512, 8192], P('seq', 'head'), may hold values from -0.25 to 0.25
- doc_lengths: int32 [128], replicated, may hold values from 1 to 510, as said below
Outputs:
- attended: bfloat16 [32768, 8192], P(('seq', 'head'))
Inputs may be any that keep to these rules, and one draw needn't show every extreme that they name: `doc_lengths`: the documents lie in order in the pack and their lengths sum to 32768; document 0 starts at position 0 and every other document d starts strictly inside positions d * 256 to (d + 1) * 256 - 1, excluding the first of these; one length is exactly 510.
All inputs are finite; a program needn't handle non-finite values.
Results may differ from a plain program's by a relative error of at most 0.0062.
Values may be sent and summed in bfloat16 or wider, within the bound.
A program may use at most 64 MiB of HBM per device.

v0:
```python
import functools
import math

import jax
import jax.numpy as jnp
from jax import lax
from jax.experimental import pallas as pl
from jax.experimental.pallas import tpu as pltpu
from jax.sharding import PartitionSpec as P

NOPE = 128
ROPE = 64
VDIM = 128
QK = NOPE + ROPE
LOG2E = 1.4426950408889634

MESH = pl.DeviceIdType.MESH


def kernel(
    sizes, queries, latrope, key_weight, value_weight, lengths, out,
    lat_all, wk, wv, qbuf, kaug, vbuf, bias, obuf,
    lat_sem, lat_send, mate_send, q_sem, q_send, w_own, w_recv, w_send, o_sem, o_send,
):
    n_seq, n_head, look, chunks, chunk_heads = sizes
    tok, rank = latrope.shape[0], latrope.shape[1] - 2 * ROPE
    rows = key_weight.shape[0]
    half = n_seq // 2
    xs = n_head // 2
    slots = look + n_head
    span = (look + 1) * tok
    cw = chunk_heads * NOPE
    qw = chunk_heads * QK
    seq, head = lax.axis_index("seq"), lax.axis_index("head")
    core, x = head % 2, head // 2
    mate = head + 1 - 2 * core

    odd = seq % 2
    place = (seq // 2) * (1 - odd) + (n_seq - 1 - seq // 2) * odd

    def at_place(where):
        where = (where + n_seq) % n_seq
        fold = where // half
        return 2 * where * (1 - fold) + (2 * (n_seq - 1 - where) + 1) * fold

    after, before = at_place(place + 1), at_place(place - 1)
    next_seq, last_seq = (seq + 1) % n_seq, (seq + n_seq - 1) % n_seq

    barrier = pltpu.get_barrier_semaphore()

    def greet(to_seq, to_head):
        pl.semaphore_signal(barrier, inc=1, device_id=(to_seq, to_head), device_id_type=MESH)

    for k in range(1, n_head):
        greet(seq, (head + k) % n_head)
    greet(after, head)
    greet(before, head)
    for k in range(xs):
        greet(next_seq, ((x + k) % xs) * 2 + core)
        greet(last_seq, ((x + k) % xs) * 2 + core)

    def own_copies():
        pltpu.make_async_copy(latrope, lat_all.at[look + head], lat_sem.at[look + head]).start()
        for c in range(chunks):
            pltpu.make_async_copy(
                queries.at[:, pl.ds(pl.multiple_of(head * chunks * qw + c * qw, 128), qw)],
                qbuf.at[c, head], q_sem.at[c, head],
            ).start()
            for kv, (source, held) in enumerate(((key_weight, wk), (value_weight, wv))):
                pltpu.make_async_copy(
                    source.at[:, pl.ds(c * cw, cw)], held.at[c, seq], w_own.at[c, kv]
                ).start()

    own_copies()
    pl.semaphore_wait(barrier, n_head - 1 + 2 + 2 * xs)

    def lat_copy(k, to_seq, slot):
        return pltpu.make_async_remote_copy(
            src_ref=latrope, dst_ref=lat_all.at[slot],
            send_sem=lat_send.at[k], recv_sem=lat_sem.at[slot],
            device_id=(to_seq, ((x + k % xs) % xs) * 2 + core), device_id_type=MESH,
        )

    def ring_parts(t):
        both = [(0, 0), (0, 1), (1, 0), (1, 1)]
        return both if t < half else [(0, 0), (1, 1)]

    def ring_copy(c, t, way, kv):
        origin = at_place(place - (t - 1)) if way == 0 else at_place(place + (t - 1))
        source, held = ((key_weight, wk), (value_weight, wv))[kv]
        src = source.at[:, pl.ds(c * cw, cw)] if t == 1 else held.at[c, origin]
        index = t - 1
        return pltpu.make_async_remote_copy(
            src_ref=src, dst_ref=held.at[c, origin],
            send_sem=w_send.at[c, index, way, kv], recv_sem=w_recv.at[c, index, way, kv],
            device_id=(after if way == 0 else before, head), device_id_type=MESH,
        )

    def ring_start(c, t):
        for way, kv in ring_parts(t):
            ring_copy(c, t, way, kv).start()

    def ring_take(c, t):
        for way, kv in ring_parts(t):
            origin = at_place(place - t) if way == 0 else at_place(place + t)
            landed = (wk, wv)[kv].at[c, origin]
            pltpu.make_async_copy(landed, landed, w_recv.at[c, t - 1, way, kv]).wait()
            if t + 1 <= half and (way, kv) in ring_parts(t + 1):
                ring_copy(c, t + 1, way, kv).start()

    def q_copy(c, k):
        peer = (head + k) % n_head
        return pltpu.make_async_remote_copy(
            src_ref=queries.at[:, pl.ds(pl.multiple_of(peer * chunks * qw + c * qw, 128), qw)],
            dst_ref=qbuf.at[c, head],
            send_sem=q_send.at[c, k - 1], recv_sem=q_sem.at[c, head],
            device_id=(seq, peer), device_id_type=MESH,
        )

    def o_copy(c, k):
        peer = (head + k) % n_head
        return pltpu.make_async_remote_copy(
            src_ref=obuf.at[c, peer],
            dst_ref=out.at[:, pl.ds(pl.multiple_of(head * chunks * cw + c * cw, 128), cw)],
            send_sem=o_send.at[c, k - 1], recv_sem=o_sem.at[c, head],
            device_id=(seq, peer), device_id_type=MESH,
        )

    def o_own(c):
        return pltpu.make_async_copy(
            obuf.at[c, head],
            out.at[:, pl.ds(pl.multiple_of(head * chunks * cw + c * cw, 128), cw)],
            o_sem.at[c, head],
        )

    for k in range(1, xs):
        lat_copy(k, seq, look + head).start()

    @pl.when(head >= n_head - look)
    def _():
        for k in range(xs):
            lat_copy(xs + k, next_seq, head - (n_head - look)).start()

    for c in range(min(2, chunks)):
        ring_start(c, 1)
    for c in range(chunks):
        for k in range(1, n_head):
            q_copy(c, k).start()

    docs = lengths.shape[0]
    later = lax.broadcasted_iota(jnp.int32, (docs, docs), 1)
    earlier = lax.broadcasted_iota(jnp.int32, (docs, docs), 0)
    starts = jnp.sum(jnp.where(earlier < later, lengths[...], 0), axis=0, keepdims=True)
    first = seq * n_head * tok

    def mask_tile(j, carry):
        q_place = first + j * tok + lax.broadcasted_iota(jnp.int32, (tok, 1), 0)
        begun = jnp.max(jnp.where(starts <= q_place, starts, 0), axis=1, keepdims=True)
        k_place = first + (j - look) * tok + lax.broadcasted_iota(jnp.int32, (tok, span), 1)
        seen = (k_place >= begun) & (k_place <= q_place)
        bias[j] = jnp.where(seen, 0.0, -jnp.inf)
        return carry

    lax.fori_loop(0, n_head, mask_tile, 0)

    def lat_wait(slot):
        pltpu.make_async_copy(lat_all.at[slot], lat_all.at[slot], lat_sem.at[slot]).wait()

    def mate_copy(i):
        slot = 2 * i + core
        return pltpu.make_async_remote_copy(
            src_ref=lat_all.at[slot], dst_ref=lat_all.at[slot],
            send_sem=mate_send.at[i], recv_sem=lat_sem.at[slot],
            device_id=(seq, mate), device_id_type=MESH,
        )

    def lat_all_in():
        for i in list(range(look // 2, slots // 2)) + list(range(look // 2)):
            lat_wait(2 * i + core)
            mate_copy(i).start()
        for i in range(slots // 2):
            lat_wait(2 * i + 1 - core)

    def rope_in():
        lane = lax.broadcasted_iota(jnp.int32, (tok, 2 * ROPE), 1)
        del lane

        def fill(slot, carry):
            tail = lat_all[slot, :, rank:]
            rolled = pltpu.roll(tail.astype(jnp.float32), ROPE, axis=1).astype(jnp.bfloat16)
            at = pl.ds(pl.multiple_of(slot * tok, tok), tok)
            for h in range(chunk_heads):
                kaug[h, at, NOPE:] = tail if h % 2 == 0 else rolled
            return carry

        lax.fori_loop(0, slots, fill, 0)

    block = slots * tok // 2

    def project(c):
        for kv in range(2):
            mine = (wk, wv)[kv].at[c, seq]
            pltpu.make_async_copy(mine, mine, w_own.at[c, kv]).wait()

        def rows_of(i, carry):
            at = pl.ds(pl.multiple_of(i * block, block), block)
            lat = lat_all[pl.ds(i * (slots // 2), slots // 2), :, :rank].reshape(block, rank)
            low = lax.broadcasted_iota(jnp.int32, (block, NOPE), 1) < ROPE
            for pair in range(chunk_heads // 2):
                cols = slice(pair * 2 * NOPE, (pair + 1) * 2 * NOPE)
                w = wk[c, :, :, cols].reshape(rank, 2 * NOPE)
                k = jnp.dot(lat, w, preferred_element_type=jnp.float32)
                kaug[2 * pair, at, :NOPE] = k[:, :NOPE].astype(jnp.bfloat16)
                turned = pltpu.roll(k[:, NOPE:], ROPE, axis=1)
                zeros_first = jnp.where(low, 0.0, turned).astype(jnp.bfloat16)
                kaug[2 * pair + 1, at, :NOPE] = zeros_first
                rope_last = kaug[2 * pair + 1, at, NOPE:].astype(jnp.float32)
                kaug[2 * pair + 1, at, NOPE:] = jnp.where(low, turned, rope_last).astype(
                    jnp.bfloat16
                )
                w = wv[c, :, :, cols].reshape(rank, 2 * VDIM)
                v = jnp.dot(lat, w, preferred_element_type=jnp.float32)
                vbuf[at, cols] = v.astype(jnp.bfloat16)
            return carry

        lax.fori_loop(0, 2, rows_of, 0)

    scale = LOG2E / math.sqrt(QK)

    def attend(c, first_tile, last_tile):
        def tile(j, carry):
            at = pl.ds(pl.multiple_of(j * tok, tok), span)
            hide = bias[j]
            for h in range(chunk_heads):
                begin = (h // 2) * 2 * QK + (h % 2) * NOPE
                q = qbuf[c, j, :, begin:begin + 2 * NOPE]
                s = lax.dot_general(
                    q, kaug[h, at, :], (((1,), (1,)), ((), ())),
                    preferred_element_type=jnp.float32,
                )
                s = s * scale + hide
                peak = jnp.max(s, axis=1, keepdims=True)
                expo = jnp.exp2(s - peak)
                total = jnp.sum(expo, axis=1, keepdims=True)
                cols = slice(h * VDIM, (h + 1) * VDIM)
                mixed = jnp.dot(
                    expo.astype(jnp.bfloat16), vbuf[at, cols],
                    preferred_element_type=jnp.float32,
                )
                obuf[c, j, :, cols] = (mixed / total).astype(jnp.bfloat16)
            return carry

        lax.fori_loop(first_tile, last_tile, tile, 0)

    def q_in(c):
        for k in range(n_head):
            sender = (head + k) % n_head
            landed = qbuf.at[c, sender]
            pltpu.make_async_copy(landed, landed, q_sem.at[c, sender]).wait()

    def give(c):
        for k in range(1, n_head):
            o_copy(c, k).start()
        o_own(c).start()

    def work_on(c):
        middle = n_head // 2

        def tiles_first():
            q_in(c)
            attend(c, 0, middle)

        def tiles_last():
            attend(c, middle, n_head)
            give(c)

        return [functools.partial(project, c), tiles_first, tiles_last]

    waiting = []
    for base in range(0, chunks, 2):
        pair = range(base, min(base + 2, chunks))
        for t in range(1, half + 1):
            for c in pair:
                ring_take(c, t)
                if t == half - 1 and c == pair[-1]:
                    for ahead in range(base + 2, min(base + 4, chunks)):
                        ring_start(ahead, 1)
                if base == 0 and t == 1 and c == pair[-1]:
                    lat_all_in()
                    rope_in()
                if waiting:
                    waiting.pop(0)()
        for c in pair:
            waiting += work_on(c)
    for step in waiting:
        step()

    for c in range(chunks):
        for k in range(n_head):
            sender = (head + k) % n_head
            landed = out.at[:, pl.ds(pl.multiple_of(sender * chunks * cw + c * cw, 128), cw)]
            pltpu.make_async_copy(landed, landed, o_sem.at[c, sender]).wait()
        for k in range(1, n_head):
            q_copy(c, k).wait_send()
            o_copy(c, k).wait_send()
        for t in range(1, half + 1):
            for way, kv in ring_parts(t):
                ring_copy(c, t, way, kv).wait_send()
    for k in range(1, xs):
        lat_copy(k, seq, look + head).wait_send()

    @pl.when(head >= n_head - look)
    def _():
        for k in range(xs):
            lat_copy(xs + k, next_seq, head - (n_head - look)).wait_send()

    for i in range(slots // 2):
        mate_copy(i).wait_send()


def shards(queries, latent, rope_keys, key_weight, value_weight, doc_lengths):
    n_seq, n_head = lax.axis_size("seq"), lax.axis_size("head")
    tok, rank = latent.shape
    rows = key_weight.shape[0]
    local_heads = key_weight.shape[1] // NOPE
    docs = doc_lengths.shape[0]
    slot_rows = n_seq * n_head * tok // docs
    look = 2 * -(-slot_rows // tok)
    chunk_heads = min(4, local_heads)
    chunks = local_heads // chunk_heads
    slots, span, half = look + n_head, (look + 1) * tok, n_seq // 2
    cw, qw = chunk_heads * NOPE, chunk_heads * QK
    latrope = jnp.concatenate(
        [latent, rope_keys, jnp.zeros((tok, 2 * ROPE - rope_keys.shape[1]), latent.dtype)], axis=1
    )
    anywhere = pl.BlockSpec(memory_space=pl.ANY)
    dma = pltpu.SemaphoreType.DMA
    bf16 = jnp.bfloat16
    return pl.pallas_call(
        functools.partial(kernel, (n_seq, n_head, look, chunks, chunk_heads)),
        out_shape=jax.ShapeDtypeStruct((tok, n_head * local_heads * VDIM), bf16),
        in_specs=[anywhere] * 4 + [pl.BlockSpec(memory_space=pltpu.VMEM)],
        out_specs=anywhere,
        scratch_shapes=[
            pltpu.VMEM((slots, tok, rank + 2 * ROPE), bf16),
            pltpu.VMEM((chunks, n_seq, rows, cw), bf16),
            pltpu.VMEM((chunks, n_seq, rows, cw), bf16),
            pltpu.VMEM((chunks, n_head, tok, qw), bf16),
            pltpu.VMEM((chunk_heads, slots * tok, 2 * NOPE), bf16),
            pltpu.VMEM((slots * tok, cw), bf16),
            pltpu.VMEM((n_head, tok, span), jnp.float32),
            pltpu.VMEM((chunks, n_head, tok, cw), bf16),
            dma((slots,)),
            dma((n_head,)),
            dma((slots // 2,)),
            dma((chunks, n_head)),
            dma((chunks, n_head - 1)),
            dma((chunks, 2)),
            dma((chunks, half, 2, 2)),
            dma((chunks, half, 2, 2)),
            dma((chunks, n_head)),
            dma((chunks, n_head - 1)),
        ],
        compiler_params=pltpu.CompilerParams(collective_id=0, has_side_effects=True),
    )(queries, latrope, key_weight, value_weight, doc_lengths.reshape(docs, 1))


def solution(mesh):
    placed = (
        P(("seq", "head"), None),
        P(("seq", "head"), None),
        P(("seq", "head"), None),
        P("seq", "head"),
        P("seq", "head"),
        P(),
    )
    return jax.shard_map(
        shards, mesh=mesh, in_specs=placed, out_specs=P(("seq", "head"), None), check_vma=False
    )
```

profile of v0, /device:TPU:1, one launch (start us, length us, event | category | flops | bytes accessed | tf_op | source)
XLA Modules:
  0.0 143.2 jit_solution(18243301948036114527)
XLA Ops:
  0.0 0.1 pad.2.clone
  0.1 0.8 copy.7
  0.9 1.4 copy.8.lengths
  2.3 1.6 %maximum_maximum_fusion.latrope = bf16[128,640]{1,0:T(8,128)(2,1)} fusion(bf16[128,64]{1,0:T(8,128)(2,1)S(1)} %copy.7, bf16[128,512]{1,0:T(8,128)(2,1)} %param.7, bf16[640]{0:T(1024)(128)(2,1)S(1)} %pad.2.clone), kind=kLoop, calls=%fused_computation | loop fusion | flops 491520 | bytes 312576 | tf_op jit(solution)/shard_map/concatenate | solution.py:333
  3.9 136.2 %shard_map.64 = bf16[128,8192]{1,0:T(8,128)(2,1)} custom-call(bf16[128,12288]{1,0:T(8,128)(2,1)} %queries.1, bf16[128,640]{1,0:T(8,128)(2,1)} %maximum_maximum_fusion.latrope, bf16[16,1024]{1,0:T(8,128)(2,1)} %key_weight.1, bf16[16,1024]{1,0:T(8,128)(2,1)} %value_weight.1, s32[128,1]{1,0:T(8,128)} %copy.8.lengths), custom_call_target="tpu_custom_call" | custom-call | tf_op jit(solution)/shard_map/pallas_call | solution.py:339
  140.1 3.1 %copy.10 = bf16[128,8192]{1,0:T(8,128)(2,1)} copy(bf16[128,8192]{1,0:T(8,128)(2,1)} %shard_map.64) | data formatting | bytes 4194304
  (1 shorter events, 0.0 us)
where the time goes:
time: 144 us; the launch traced here: 143 us
  Pallas kernels  136 us (94%)
  local copies, waits for them, and re-layouts  5.39 us (4%)
  other arithmetic  1.6 us (1%)
    pallas_call x1, Pallas kernels, shards(): pl.pallas_call(functools.partial(kernel, (n_seq, n_head, look, chunks, ch...  136 us
    unnamed x2, local copies, waits for them, and re-layouts  3.92 us

commit v1 on v0

v1 whole, which is shorter than its diff:
```python
import functools
import math

import jax
import jax.numpy as jnp
from jax import lax
from jax.experimental import pallas as pl
from jax.experimental.pallas import tpu as pltpu
from jax.sharding import PartitionSpec as P

NOPE = 128
ROPE = 64
VDIM = 128
QK = NOPE + ROPE
LOG2E = 1.4426950408889634
NY = 4

MESH = pl.DeviceIdType.MESH

FINE = (True, False, False, True)
RATE = 46.6e3
LATENCY = 2.3
HOP = 0.8
D2D_RATE = 300e3
BACKLOG = 1.5
SEND_COST = 0.04
WAIT_COST = 0.02
PIECE = (0.55, 0.45)


class Message:
    def __init__(self, name, deps, link, size, priority, units=None, where=None, move=None, hops=1):
        self.name, self.deps, self.link, self.size = name, deps, link, size
        self.priority, self.units, self.where, self.move, self.hops = priority, units, where, move, hops


def weight_messages(stages, nx, nz):
    tile = 16 * 128 * 2
    found = []

    def add(name, deps, axis, step, units, where, priority, blocks):
        move = {"x": 0, "z": 0, "y": 0}
        move[axis] = step
        hops = 2 if abs(step) == 2 else 1
        link = axis + ("+" if step > 0 else "-")
        found.append(
            Message(name, deps, link, blocks * units[1] * tile, priority, units, where, move, hops)
        )

    half = nz // 2
    for s in range(stages):
        for flow, (minor, last) in enumerate((("y", "x"), ("x", "y"))):
            both = (4 * s + 2 * flow, 2)
            first, second = (both[0], 1), (both[0] + 1, 1)

            def at(minor_at, last_at, z_at):
                return {minor: minor_at, last: last_at, "z": z_at}

            key = (s, flow)
            for k in (1, -1, 2):
                add((*key, "near", k), [], minor, k, both, at(0, 0, 0), (0, s), 1)
            near = [(*key, "near", k) for k in (1, -1, 2)]
            plus_far = s % 2 == 0
            reach = {1: half if plus_far else half - 1, -1: half - 1 if plus_far else half}
            came = {0: near}
            for way in (1, -1):
                for d in range(1, reach[way] + 1):
                    deps = near if d == 1 else [(*key, "z", way, d - 1)]
                    add((*key, "z", way, d), deps, "z", way, both, at(None, 0, -way * (d - 1)), (s, 0), 4)
                    came[-way * d] = [(*key, "z", way, d)]
            every = [name for names in came.values() for name in names]
            add((*key, "far"), near, last, 2, second, at(None, 0, 0), (s, 1), 4)
            for way in (1, -1):
                for d in range(1, reach[way] + 1):
                    deps = [(*key, "far")] if d == 1 else [(*key, "farz", way, d - 1)]
                    add((*key, "farz", way, d), deps, "z", way, second, at(None, 2, -way * (d - 1)), (s, 2), 4)
            if FINE[s]:
                for r, deps in came.items():
                    for way in (1, -1):
                        add((*key, "side", way, r), deps, last, way, both, at(None, 0, r), (s, 3), 4)
                    via = 1 if r in (0, -1, -2, -3) else -1
                    add(
                        (*key, "over", via, r), [(*key, "side", via, r)], last, via, first,
                        at(None, -via, r), (s, 2), 4,
                    )
            else:
                for way in (1, -1):
                    add((*key, "side", way), every, last, way, both, at(None, 0, None), (s, 3), 4 * nz)
                for way, part in ((1, (0, half)), (-1, (half, nz))):
                    add(
                        (*key, "over", way), [(*key, "side", way)], last, way, first,
                        at(None, -way, part), (s, 2), 4 * half,
                    )
    return found


def latent_messages(tok, rank):
    size = tok * (rank + 2 * ROPE) * 2
    return [
        Message(("next",), [], "x+", size, (0, 9), hops=1.5),
        Message(("mate",), [], "d2d", size, (0, 9)),
        Message(("share",), [("next",)], "d2d", size, (0, 9)),
    ]


def step_needs(messages, s, off):
    names = [m.name for m in messages if len(m.name) > 2]
    values = [n for n in names if n[0] == s and n[1] == 1]
    own = [n for n in names if n[0] == s and n[1] == 0 and n[2] in ("near", "z")]
    sides = {
        way: [n for n in names if n[0] == s and n[1] == 0 and n[2] == "side" and n[3] == way]
        for way in (1, -1)
    }
    opposite = [n for n in names if n[0] == s and n[1] == 0 and n[2] in ("over", "far", "farz")]
    return values + {0: own, -1: sides[1], 1: sides[-1], 2: opposite}[off]


OFFSETS = (0, -1, 1, 2)


def make_plan(messages, stages):
    by_name = {m.name: m for m in messages}
    pieces = [("setup", [("next",), ("mate",), ("share",)], 0.8)]
    for s in range(stages):
        for off in OFFSETS:
            for p, length in enumerate(PIECE):
                pieces.append(((s, off, p), step_needs(messages, s, off) if p == 0 else [], length))
    order, free, arrive, seen = [], {}, {}, set()
    waiting = sorted(messages, key=lambda m: m.priority)
    now, at_piece = 0.0, 0
    while waiting or arrive or at_piece < len(pieces):
        landed = sorted((t, str(n), n) for n, t in arrive.items() if t <= now)
        if landed:
            name = landed[0][2]
            del arrive[name]
            seen.add(name)
            order.append(("wait", name))
            now += WAIT_COST
            continue
        ready = [m for m in waiting if all(d in seen for d in m.deps)]
        able = [m for m in ready if free.get(m.link, 0.0) - now < BACKLOG]
        if able:
            m = able[0]
            waiting.remove(m)
            order.append(("send", m.name))
            now += SEND_COST
            rate = D2D_RATE if m.link == "d2d" else RATE
            begun = max(now, free.get(m.link, 0.0))
            free[m.link] = begun + m.size * max(1, m.hops) / rate
            arrive[m.name] = free[m.link] + LATENCY + HOP * (m.hops - 1)
            continue
        if at_piece < len(pieces) and all(n in seen for n in pieces[at_piece][1]):
            order.append(("piece", pieces[at_piece][0]))
            now += pieces[at_piece][2]
            at_piece += 1
            continue
        times = list(arrive.values()) + [free[m.link] - BACKLOG for m in ready]
        now = max(now, min(times)) + 1e-6
    return order, now


def kernel(
    sizes, queries, latent, key_weight, value_weight, lengths, out,
    w, lat, qbuf, kaug, rope_odd, vbuf, bias, obuf, len_buf,
    own_sem, lat_sem, len_sem, lat_send, w_recv, w_send, q_sem, q_send, o_sem, o_send, o_own,
):
    n_seq, n_head, stages = sizes
    nx, ny, nz = n_head // 2, NY, n_seq // NY
    tok, rank = latent.shape[0], latent.shape[1] - 2 * ROPE
    keys = 4 * tok
    seq, head = lax.axis_index("seq"), lax.axis_index("head")
    x, core = head // 2, head % 2
    z, y = seq // ny, seq % ny
    mate = 2 * x + 1 - core
    slot = seq * nx + x
    after, before = (slot + 1) % (n_seq * nx), (slot + n_seq * nx - 1) % (n_seq * nx)

    messages = weight_messages(stages, nx, nz) + latent_messages(tok, rank)
    order, _ = make_plan(messages, stages)
    by_name = {m.name: m for m in messages}
    number = {m.name: i for i, m in enumerate(messages)}

    def device(dx, dy, dz):
        return ((z + dz) % nz) * ny + (y + dy) % ny, ((x + dx) % nx) * 2 + core

    def chip(which):
        return which // nx, (which % nx) * 2 + core

    barrier = pltpu.get_barrier_semaphore()
    peers = [device(k, 0, 0) for k in range(1, nx)] + [device(0, k, 0) for k in range(1, ny)]
    peers += [device(0, 0, 1), device(0, 0, nz - 1), (seq, mate), chip(after), chip(before)]
    for peer in peers:
        pl.semaphore_signal(barrier, inc=1, device_id=peer, device_id_type=MESH)

    for s in range(stages):
        for kv, source in enumerate((key_weight, value_weight)):
            for j in range(2):
                pltpu.make_async_copy(
                    source.at[:, pl.ds((2 * s + j) * 128, 128)],
                    w.at[4 * s + 2 * kv + j, x, z, y], own_sem.at[s],
                ).start()
    pltpu.make_async_copy(latent, lat.at[2 + core], lat_sem.at[2 + core]).start()
    length_copy = pltpu.make_async_copy(lengths, len_buf, len_sem.at[0])
    length_copy.start()
    qw, cw = 2 * stages * QK, 2 * stages * VDIM

    def q_part(to_core, xi):
        return queries.at[:, pl.ds(pl.multiple_of((2 * xi + to_core) * qw, 128), qw)]

    for xi in range(nx):
        pltpu.make_async_copy(q_part(core, xi), qbuf.at[core, xi], q_sem.at[core, xi]).start()

    for s in range(stages):
        landed = w.at[pl.ds(4 * s, 4), x, z, y]
        pltpu.make_async_copy(landed, landed, own_sem.at[s]).wait()
    pl.semaphore_wait(barrier, len(peers))

    def place(at, here, n):
        if at is None:
            return pl.ds(0, n)
        if isinstance(at, tuple):
            return pl.ds(at[0], at[1] - at[0])
        return (here + at % n) % n

    def block(m, sent):
        back = {a: 0 if sent else m.move[a] for a in "xyz"}

        def shifted(a):
            at = m.where[a]
            return at - back[a] if isinstance(at, int) else at

        return w.at[
            pl.ds(*m.units), place(shifted("x"), x, nx), place(shifted("z"), z, nz), place(shifted("y"), y, ny)
        ]

    def copy_of(name):
        m = by_name[name]
        if name == ("next",):
            return pltpu.make_async_remote_copy(
                src_ref=latent, dst_ref=lat.at[core], send_sem=lat_send.at[0],
                recv_sem=lat_sem.at[core], device_id=chip(after), device_id_type=MESH,
            )
        if name == ("mate",):
            return pltpu.make_async_remote_copy(
                src_ref=latent, dst_ref=lat.at[2 + core], send_sem=lat_send.at[1],
                recv_sem=lat_sem.at[2 + core], device_id=(seq, mate), device_id_type=MESH,
            )
        if name == ("share",):
            return pltpu.make_async_remote_copy(
                src_ref=lat.at[core], dst_ref=lat.at[core], send_sem=lat_send.at[2],
                recv_sem=lat_sem.at[core], device_id=(seq, mate), device_id_type=MESH,
            )
        sent = block(m, True)
        i = number[name]
        return pltpu.make_async_remote_copy(
            src_ref=sent, dst_ref=sent, send_sem=w_send.at[i], recv_sem=w_recv.at[i],
            device_id=device(m.move["x"], m.move["y"], m.move["z"]), device_id_type=MESH,
        )

    def lat_wait(at):
        pltpu.make_async_copy(lat.at[at], lat.at[at], lat_sem.at[at]).wait()

    def take(name):
        if name == ("next",):
            lat_wait(core)
        elif name == ("mate",):
            lat_wait(3 - core)
        elif name == ("share",):
            lat_wait(1 - core)
        else:
            landed = block(by_name[name], False)
            pltpu.make_async_copy(landed, landed, w_recv.at[number[name]]).wait()

    def q_copy(xi):
        return pltpu.make_async_remote_copy(
            src_ref=q_part(1 - core, xi), dst_ref=qbuf.at[core, xi], send_sem=q_send.at[xi],
            recv_sem=q_sem.at[core, xi], device_id=(seq, mate), device_id_type=MESH,
        )

    def setup():
        lat_wait(2 + core)
        length_copy.wait()
        lane = lax.broadcasted_iota(jnp.int32, (1, lengths.shape[1]), 1)
        start_own = jnp.sum(jnp.where(lane < slot, len_buf[...], 0), axis=1, keepdims=True)
        start_last = jnp.sum(jnp.where(lane < slot - 1, len_buf[...], 0), axis=1, keepdims=True)
        first = slot * 2 * tok
        q_place = first + lax.broadcasted_iota(jnp.int32, (2 * tok, 1), 0)
        begun = jnp.where(q_place >= start_own, start_own, start_last)
        k_place = first - 2 * tok + lax.broadcasted_iota(jnp.int32, (2 * tok, keys), 1)
        bias[...] = jnp.where((k_place >= begun) & (k_place <= q_place), 0.0, -jnp.inf)
        tail = lat[:, :, rank:].reshape(keys, 2 * ROPE)
        kaug[0, :, NOPE:] = tail
        rope_odd[...] = pltpu.roll(tail.astype(jnp.float32), ROPE, axis=1)
        for xi in range(nx):
            for t in range(2):
                pltpu.make_async_copy(qbuf.at[t, xi], qbuf.at[t, xi], q_sem.at[t, xi]).wait()

    scale = LOG2E / math.sqrt(QK)

    def weights(s, j, xi):
        parts = [w[4 * s + j + i, xi].reshape(n_seq * 16, 128) for i in range(2)]
        return jnp.concatenate(parts, axis=1)

    def project(s, xi):
        tokens = lat[:, :, :rank].reshape(keys, rank)
        low = lax.broadcasted_iota(jnp.int32, (keys, NOPE), 1) < ROPE
        k = jnp.dot(tokens, weights(s, 0, xi), preferred_element_type=jnp.float32)
        kaug[0, :, :NOPE] = k[:, :NOPE].astype(jnp.bfloat16)
        turned = pltpu.roll(k[:, NOPE:], ROPE, axis=1)
        kaug[1, :, :NOPE] = jnp.where(low, 0.0, turned).astype(jnp.bfloat16)
        kaug[1, :, NOPE:] = jnp.where(low, turned, rope_odd[...]).astype(jnp.bfloat16)
        v = jnp.dot(tokens, weights(s, 2, xi), preferred_element_type=jnp.float32)
        vbuf[...] = v.astype(jnp.bfloat16)

    def attend(s, xi):
        for t in range(2):
            span = (3 + t) * tok
            hide = bias[t * tok:(t + 1) * tok, :span]
            for h in range(2):
                begin = pl.multiple_of(s * 2 * QK + h * NOPE, 128)
                q = qbuf[t, xi, :, pl.ds(begin, 2 * NOPE)]
                sc = lax.dot_general(
                    q, kaug[h, :span, :], (((1,), (1,)), ((), ())),
                    preferred_element_type=jnp.float32,
                )
                sc = sc * scale + hide
                peak = jnp.max(sc, axis=1, keepdims=True)
                expo = jnp.exp2(sc - peak)
                total = jnp.sum(expo, axis=1, keepdims=True)
                cols = slice(h * VDIM, (h + 1) * VDIM)
                mixed = jnp.dot(
                    expo.astype(jnp.bfloat16), vbuf[:span, cols],
                    preferred_element_type=jnp.float32,
                )
                obuf[t, s, xi, :, cols] = (mixed / total).astype(jnp.bfloat16)

    def out_part(s, xi):
        at = pl.multiple_of((2 * xi + core) * cw + s * 2 * VDIM, 128)
        return out.at[:, pl.ds(at, 2 * VDIM)]

    def give_own(s, xi):
        return pltpu.make_async_copy(obuf.at[core, s, xi], out_part(s, xi), o_own.at[s, xi])

    def give_mate(s, xi):
        return pltpu.make_async_remote_copy(
            src_ref=obuf.at[1 - core, s, xi], dst_ref=out_part(s, xi), send_sem=o_send.at[s, xi],
            recv_sem=o_sem.at[s, xi], device_id=(seq, mate), device_id_type=MESH,
        )

    def act(kind, name):
        if kind == "send":
            copy_of(name).start()
        else:
            take(name)

    prologue, slots, current = [], {}, None
    for kind, name in order:
        if kind == "piece" and name != "setup":
            s, off, p = name
            current = (s * nx + OFFSETS.index(off), p)
            slots[current] = []
        elif current is None:
            prologue.append((kind, name))
        else:
            slots[current].append((kind, name))

    for kind, name in prologue:
        if kind == "piece":
            for xi in range(nx):
                q_copy(xi).start()
            setup()
        else:
            act(kind, name)

    def step(i, carry):
        s, turn = i // nx, i % nx
        off = jnp.where(turn == 0, 0, jnp.where(turn == 1, nx - 1, jnp.where(turn == 2, 1, 2)))
        xi = (x + off) % nx

        def events(p, low, high):
            if not any(slots[(k, p)] for k in range(low, high)):
                return
            if high - low == 1:
                for kind, name in slots[(low, p)]:
                    act(kind, name)
                return
            middle = (low + high) // 2
            pl.when(i < middle)(functools.partial(events, p, low, middle))
            pl.when(i >= middle)(functools.partial(events, p, middle, high))

        project(s, xi)
        events(0, 0, stages * nx)
        attend(s, xi)
        give_own(s, xi).start()
        give_mate(s, xi).start()
        events(1, 0, stages * nx)
        return carry

    lax.fori_loop(0, stages * nx, step, 0)

    def close(i, carry):
        s, xi = i // nx, i % nx
        give_own(s, xi).wait()
        give_mate(s, xi).wait_send()
        landed = out_part(s, xi)
        at = pl.multiple_of((2 * xi + core) * cw + s * 2 * VDIM, 128)
        del at
        pltpu.make_async_copy(landed, landed, o_sem.at[s, xi]).wait()
        return carry

    for xi in range(nx):
        q_copy(xi).wait_send()
    for m in messages:
        copy_of(m.name).wait_send()
    lax.fori_loop(0, stages * nx, close, 0)


def shards(queries, latent, rope_keys, key_weight, value_weight, doc_lengths):
    n_seq, n_head = lax.axis_size("seq"), lax.axis_size("head")
    nx = n_head // 2
    tok, rank = latent.shape
    stages = key_weight.shape[1] // (2 * NOPE)
    docs = doc_lengths.shape[0]
    latrope = jnp.concatenate(
        [latent, rope_keys, jnp.zeros((tok, 2 * ROPE - rope_keys.shape[1]), latent.dtype)], axis=1
    )
    count = len(weight_messages(stages, nx, n_seq // NY)) + 3
    anywhere = pl.BlockSpec(memory_space=pl.ANY)
    dma = pltpu.SemaphoreType.DMA
    bf16 = jnp.bfloat16
    return pl.pallas_call(
        functools.partial(kernel, (n_seq, n_head, stages)),
        out_shape=jax.ShapeDtypeStruct((tok, n_head * stages * 2 * VDIM), bf16),
        in_specs=[anywhere] * 5,
        out_specs=anywhere,
        scratch_shapes=[
            pltpu.VMEM((4 * stages, nx, n_seq // NY, NY, key_weight.shape[0], 128), bf16),
            pltpu.VMEM((4, tok, rank + 2 * ROPE), bf16),
            pltpu.VMEM((2, nx, tok, 2 * stages * QK), bf16),
            pltpu.VMEM((2, 4 * tok, 2 * NOPE), bf16),
            pltpu.VMEM((4 * tok, 2 * ROPE), jnp.float32),
            pltpu.VMEM((4 * tok, 2 * VDIM), bf16),
            pltpu.VMEM((2 * tok, 4 * tok), jnp.float32),
            pltpu.VMEM((2, stages, nx, tok, 2 * VDIM), bf16),
            pltpu.VMEM((1, docs), jnp.int32),
            dma((stages,)),
            dma((4,)),
            dma((1,)),
            dma((3,)),
            dma((count,)),
            dma((count,)),
            dma((2, nx)),
            dma((nx,)),
            dma((stages, nx)),
            dma((stages, nx)),
            dma((stages, nx)),
        ],
        compiler_params=pltpu.CompilerParams(collective_id=0, has_side_effects=True),
    )(queries, latrope, key_weight, value_weight, doc_lengths.reshape(1, docs))


def solution(mesh):
    placed = (
        P(("seq", "head"), None),
        P(("seq", "head"), None),
        P(("seq", "head"), None),
        P("seq", "head"),
        P("seq", "head"),
        P(),
    )
    return jax.shard_map(
        shards, mesh=mesh, in_specs=placed, out_specs=P(("seq", "head"), None), check_vma=False
    )
```

time: 144 us -> 91.2 us (0.63)
  Pallas kernels: 136 us -> 85.4 us
    pallas_call x1, Pallas kernels: 136 us -> 85.4 us  [shards(): pl.pallas_call(functools.partial(kernel, (n_seq, n_head, stages)), out_sh...]
where the time goes in v1:
time: 91.2 us; the launch traced here: 91 us
  Pallas kernels  85.4 us (94%)
  local copies, waits for them, and re-layouts  4 us (4%)
  other arithmetic  1.61 us (2%)
    pallas_call x1, Pallas kernels, shards(): pl.pallas_call(functools.partial(kernel, (n_seq, n_head, stages)), out_sh...  85.4 us
    unnamed x2, local copies, waits for them, and re-layouts  3.92 us

profile of v1, /device:TPU:1, one launch (start us, length us, event | category | flops | bytes accessed | tf_op | source)
XLA Modules:
  0.0 91.0 jit_solution(6232720006182083007)
XLA Ops:
  0.0 0.1 pad.2.clone
  0.1 0.8 copy.7
  0.9 1.6 %maximum_maximum_fusion.latent = bf16[128,640]{1,0:T(8,128)(2,1)} fusion(bf16[128,64]{1,0:T(8,128)(2,1)S(1)} %copy.7, bf16[128,512]{1,0:T(8,128)(2,1)} %param.7, bf16[640]{0:T(1024)(128)(2,1)S(1)} %pad.2.clone), kind=kLoop, calls=%fused_computation | loop fusion | flops 491520 | bytes 312576 | tf_op jit(solution)/shard_map/concatenate | solution.py:424
  2.5 85.4 %shard_map.64 = bf16[128,8192]{1,0:T(8,128)(2,1)} custom-call(bf16[128,12288]{1,0:T(8,128)(2,1)} %queries.1, bf16[128,640]{1,0:T(8,128)(2,1)} %maximum_maximum_fusion.latent, bf16[16,1024]{1,0:T(8,128)(2,1)} %key_weight.1, bf16[16,1024]{1,0:T(8,128)(2,1)} %value_weight.1, s32[1,128]{1,0:T(1,128)} %bitcast.1), custom_call_target="tpu_custom_call" | custom-call | tf_op jit(solution)/shard_map/pallas_call | solution.py:431
  87.9 3.1 %copy.9 = bf16[128,8192]{1,0:T(8,128)(2,1)} copy(bf16[128,8192]{1,0:T(8,128)(2,1)} %shard_map.64) | data formatting | bytes 4194304
  (1 shorter events, 0.0 us)

commit v2 on v1

v2 whole, which is shorter than its diff:
```python
import functools
import math

import jax
import jax.numpy as jnp
from jax import lax
from jax.experimental import pallas as pl
from jax.experimental.pallas import tpu as pltpu
from jax.sharding import PartitionSpec as P

NOPE = 128
ROPE = 64
VDIM = 128
QK = NOPE + ROPE
LOG2E = 1.4426950408889634
NY = 4

MESH = pl.DeviceIdType.MESH

STAGES = (("x", 0), ("y", 4), ("y", 2), ("x", 4))
UNITS = 4
RATE = 46.6e3
LATENCY = 2.3
HOP = 0.8
D2D_RATE = 300e3
BACKLOG = 0.7
SEND_COST = 0.04
WAIT_COST = 0.02
LENGTH = {"first": 0.4, "both": 0.9, "last": 0.6, "setup": 0.8}
OFFSETS = (0, -1, 1, 2)


class Message:
    def __init__(self, name, group, kind, deps, link, size, priority, units=None, where=None, move=None, hops=1):
        self.name, self.group, self.kind, self.deps, self.link = name, group, kind, deps, link
        self.size, self.priority, self.units, self.where = size, priority, units, where
        self.move, self.hops = move, hops


def weight_messages(nx, nz):
    tile = 16 * 128 * 2
    half = nz // 2
    found = []

    def add(name, group, kind, deps, axis, step, units, where, priority, blocks):
        move = {"x": 0, "z": 0, "y": 0}
        move[axis] = step
        link = axis + ("+" if step > 0 else "-")
        found.append(Message(
            name, group, kind, deps, link, blocks * units[1] * tile, priority, units, where, move, abs(step)
        ))

    for s, (last, count) in enumerate(STAGES):
        minor = "y" if last == "x" else "x"
        every, far, over = (UNITS * s, UNITS), (UNITS * s, count), (UNITS * s + count, UNITS - count)

        def at(minor_at, last_at, z_at):
            return {minor: minor_at, last: last_at, "z": z_at}

        near = [(s, "near", k) for k in (1, -1, 2)]
        for k in (1, -1, 2):
            add((s, "near", k), (s, "near"), "near", [], minor, k, every, at(0, 0, 0), (0, s), 1)
        reach = {1: half - s % 2, -1: half - 1 + s % 2}
        came = {0: near}
        for way in (1, -1):
            for d in range(1, reach[way] + 1):
                deps = near if d == 1 else [(s, "z", way, d - 1)]
                name = (s, "z", way, d)
                add(name, name, "z", deps, "z", way, every, at(None, 0, -way * (d - 1)), (s, 0), 4)
                came[-way * d] = [name]
        if count:
            name = (s, "far")
            add(name, name, "far", near, last, 2, far, at(None, 0, 0), (s, 1), 4)
            for way in (1, -1):
                for d in range(1, reach[way] + 1):
                    deps = [(s, "far")] if d == 1 else [(s, "farz", way, d - 1)]
                    name = (s, "farz", way, d)
                    add(name, name, "far", deps, "z", way, far, at(None, 2, -way * (d - 1)), (s, 2), 4)
        for r, deps in came.items():
            via = 1 if r in (0, -1, -2, -3) else -1
            for way in (1, -1):
                name = (s, "side", way, r)
                relayed = way == via and count < UNITS
                group = name if relayed else (s, "side", way, "rest")
                add(name, group, "side", deps, last, way, every, at(None, 0, r), (s, 3), 4)
                if relayed:
                    add(
                        (s, "over", way, r), (s, "over", way), "over", [name], last, way, over,
                        at(None, -way, r), (s, 2), 4,
                    )
    return found


def latent_messages(tok, rank):
    size = tok * (rank + ROPE) * 2
    return [
        Message(("next",), ("next",), "latent", [], "x+", size, (0, 9), hops=1.5),
        Message(("mate",), ("mate",), "latent", [], "d2d", size, (0, 9)),
        Message(("share",), ("share",), "latent", [("next",)], "d2d", size, (0, 9)),
    ]


def step_needs(messages, s, off):
    groups = {m.group for m in messages if m.name[0] == s}
    if STAGES[s][0] == "y":
        return groups
    if off == 0:
        return {g for g in groups if g[1] in ("near", "z")}
    if off in (-1, 1):
        return {g for g in groups if g[1] == "side" and g[2] == -off}
    return {g for g in groups if g[1] in ("over", "far", "farz")}


def make_plan(messages):
    pieces = [("setup", {("next",), ("mate",), ("share",)})]
    steps = [(s, off) for s in range(len(STAGES)) for off in OFFSETS]
    for k, (s, off) in enumerate(steps):
        kind = "first" if k == 0 else "both"
        if k == len(steps) - 1:
            pieces.append((("last", k - 1), set()))
            kind = "first"
        pieces.append(((kind, k), step_needs(messages, s, off)))
    pieces.append((("last", len(steps) - 1), set()))
    group_of = {m.name: m.group for m in messages}
    left = {}
    for m in messages:
        left[m.group] = left.get(m.group, 0) + 1
    order, free, flying, seen = [], {}, [], set()
    waiting = sorted(messages, key=lambda m: m.priority)
    now, at_piece = 0.0, 0
    while waiting or flying or at_piece < len(pieces):
        flying.sort(key=lambda f: f[:2])
        if flying and flying[0][0] <= now:
            group = flying.pop(0)[2]
            left[group] -= 1
            if left[group] == 0:
                seen.add(group)
                order.append(("wait", group))
                now += WAIT_COST
            continue
        ready = [m for m in waiting if all(group_of[d] in seen for d in m.deps)]
        able = [m for m in ready if free.get(m.link, 0.0) - now < BACKLOG]
        if able:
            m = able[0]
            waiting.remove(m)
            order.append(("send", m.name))
            now += SEND_COST
            rate = D2D_RATE if m.link == "d2d" else RATE
            begun = max(now, free.get(m.link, 0.0))
            free[m.link] = begun + m.size * max(1, m.hops) / rate
            flying.append((free[m.link] + LATENCY + HOP * (m.hops - 1), len(order), m.group))
            continue
        if at_piece < len(pieces) and pieces[at_piece][1] <= seen:
            name = pieces[at_piece][0]
            order.append(("piece", name))
            now += LENGTH[name if name == "setup" else name[0]]
            at_piece += 1
            continue
        times = [f[0] for f in flying[:1]] + [free[m.link] - BACKLOG for m in ready]
        now = max(now, min(times)) + 1e-6
    return order, now


SEND_KINDS = ("near", "z", "far", "side", "over")


def kernel(
    sizes, queries, latent, rope, key_weight, value_weight, lengths, out,
    w, lat, rope_all, qbuf, kaug0, kaug1, rope_odd, vbuf0, vbuf1, bias, obuf, len_buf,
    own_sem, lat_sem, rope_sem, len_sem, lat_send, w_recv, w_send, q_sem, q_send, o_sem,
):
    n_seq, n_head, stages = sizes
    nx, ny, nz = n_head // 2, NY, n_seq // NY
    tok, rank = latent.shape
    keys = 4 * tok
    seq, head = lax.axis_index("seq"), lax.axis_index("head")
    x, core = head // 2, head % 2
    z, y = seq // ny, seq % ny
    mate = 2 * x + 1 - core
    slot = seq * nx + x
    after, before = (slot + 1) % (n_seq * nx), (slot + n_seq * nx - 1) % (n_seq * nx)

    messages = weight_messages(nx, nz)
    every = messages + latent_messages(tok, rank)
    order, _ = make_plan(every)
    by_name = {m.name: m for m in every}
    groups = list(dict.fromkeys(m.group for m in messages))
    number = {g: i for i, g in enumerate(groups)}
    members = {g: [m for m in messages if m.group == g] for g in groups}
    sent_tiles = {kind: sum(m.size for m in messages if m.kind == kind) // 4096 for kind in SEND_KINDS}

    def device(dx, dy, dz):
        return ((z + dz) % nz) * ny + (y + dy) % ny, ((x + dx) % nx) * 2 + core

    def chip(which):
        return which // nx, (which % nx) * 2 + core

    barrier = pltpu.get_barrier_semaphore()
    peers = [device(k, 0, 0) for k in range(1, nx)] + [device(0, k, 0) for k in range(1, ny)]
    peers += [device(0, 0, 1), device(0, 0, nz - 1), (seq, mate), chip(after), chip(before)]
    for peer in peers:
        pl.semaphore_signal(barrier, inc=1, device_id=peer, device_id_type=MESH)

    for s in range(stages):
        for kv, source in enumerate((key_weight, value_weight)):
            for j in range(2):
                pltpu.make_async_copy(
                    source.at[:, pl.ds((2 * s + j) * 128, 128)],
                    w.at[UNITS * s + 2 * kv + j, x, z, y], own_sem.at[0],
                ).start()
    pltpu.make_async_copy(latent, lat.at[2 + core], lat_sem.at[2 + core]).start()
    pltpu.make_async_copy(rope, rope_all.at[2 + core], rope_sem.at[2 + core]).start()
    length_copy = pltpu.make_async_copy(lengths, len_buf, len_sem.at[0])
    length_copy.start()
    qw, cw = 2 * stages * QK, 2 * stages * VDIM

    def q_part(to_core, xi):
        return queries.at[:, pl.ds(pl.multiple_of((2 * xi + to_core) * qw, 128), qw)]

    for xi in range(nx):
        pltpu.make_async_copy(q_part(core, xi), qbuf.at[core, xi], q_sem.at[core]).start()

    def tiles(count):
        a, b, c, d = w.shape[:4]
        for k in range(1, d + 1):
            for j in range(1, c + 1):
                for i in range(1, b + 1):
                    if count % (i * j * k) == 0 and count // (i * j * k) <= a:
                        return w.at[pl.ds(0, count // (i * j * k)), pl.ds(0, i), pl.ds(0, j), pl.ds(0, k)]
        raise ValueError(count)

    def await_bytes(ref, sem):
        pltpu.make_async_copy(ref, ref, sem).wait()

    await_bytes(w.at[:, x, z, y], own_sem.at[0])
    pl.semaphore_wait(barrier, len(peers))

    def place(at, here, n):
        return pl.ds(0, n) if at is None else (here + at % n) % n

    def block(m, sent):
        def shifted(a):
            at = m.where[a]
            return at if at is None or sent else at - m.move[a]

        return w.at[
            pl.ds(*m.units), place(shifted("x"), x, nx), place(shifted("z"), z, nz), place(shifted("y"), y, ny)
        ]

    def remote(src, dst, send_sem, recv_sem, to):
        return pltpu.make_async_remote_copy(
            src_ref=src, dst_ref=dst, send_sem=send_sem, recv_sem=recv_sem,
            device_id=to, device_id_type=MESH,
        )

    def latent_copies(name):
        at = 2 + core if name == ("mate",) else core
        to = chip(after) if name == ("next",) else (seq, mate)
        shared = name == ("share",)
        return [
            remote(
                held.at[at] if shared else mine, held.at[at], lat_send.at[0], sems.at[at], to
            )
            for mine, held, sems in ((latent, lat, lat_sem), (rope, rope_all, rope_sem))
        ]

    def send(name):
        m = by_name[name]
        if m.kind == "latent":
            for copy in latent_copies(name):
                copy.start()
            return
        sent = block(m, True)
        remote(
            sent, sent, w_send.at[SEND_KINDS.index(m.kind)], w_recv.at[number[m.group]],
            device(m.move["x"], m.move["y"], m.move["z"]),
        ).start()

    def lat_wait(at):
        await_bytes(lat.at[at], lat_sem.at[at])
        await_bytes(rope_all.at[at], rope_sem.at[at])

    def take(group):
        if group == ("next",):
            lat_wait(core)
        elif group == ("mate",):
            lat_wait(3 - core)
        elif group == ("share",):
            lat_wait(1 - core)
        elif len(members[group]) == 1:
            await_bytes(block(members[group][0], False), w_recv.at[number[group]])
        else:
            count = sum(m.size for m in members[group]) // 4096
            await_bytes(tiles(count), w_recv.at[number[group]])

    def q_copy(xi):
        return remote(
            q_part(1 - core, xi), qbuf.at[core, xi], q_send.at[0], q_sem.at[core], (seq, mate)
        )

    def setup():
        lat_wait(2 + core)
        length_copy.wait()
        lane = lax.broadcasted_iota(jnp.int32, (1, lengths.shape[1]), 1)
        start_own = jnp.sum(jnp.where(lane < slot, len_buf[...], 0), axis=1, keepdims=True)
        start_last = jnp.sum(jnp.where(lane < slot - 1, len_buf[...], 0), axis=1, keepdims=True)
        first = slot * 2 * tok
        q_place = first + lax.broadcasted_iota(jnp.int32, (2 * tok, 1), 0)
        begun = jnp.where(q_place >= start_own, start_own, start_last)
        k_place = first - 2 * tok + lax.broadcasted_iota(jnp.int32, (2 * tok, keys), 1)
        bias[...] = jnp.where((k_place >= begun) & (k_place <= q_place), 0.0, -jnp.inf)
        for at in range(4):
            turned = rope_all[at].astype(jnp.float32)
            tail = jnp.concatenate([turned, jnp.zeros_like(turned)], axis=0).T
            rows = slice(at * tok, (at + 1) * tok)
            for kaug in (kaug0, kaug1):
                kaug[0, rows, NOPE:] = tail.astype(jnp.bfloat16)
            rope_odd[rows, :] = pltpu.roll(tail, ROPE, axis=1)
        for t in range(2):
            await_bytes(qbuf.at[t], q_sem.at[t])

    scale = LOG2E / math.sqrt(QK)
    held = ((kaug0, vbuf0), (kaug1, vbuf1))

    def where(k):
        s, turn = k // nx, k % nx
        if isinstance(k, int):
            return s, (x + OFFSETS[turn] % nx) % nx
        off = jnp.where(turn == 0, 0, jnp.where(turn == 1, nx - 1, jnp.where(turn == 2, 1, 2)))
        return s, (x + off) % nx

    def weights(s, j, xi):
        parts = [w[UNITS * s + j + i, xi].reshape(n_seq * 16, 128) for i in range(2)]
        return jnp.concatenate(parts, axis=1)

    def project(k, parity):
        s, xi = where(k)
        kaug, vbuf = held[parity]
        tokens = lat[...].reshape(keys, rank)
        low = lax.broadcasted_iota(jnp.int32, (keys, NOPE), 1) < ROPE
        k = jnp.dot(tokens, weights(s, 0, xi), preferred_element_type=jnp.float32)
        kaug[0, :, :NOPE] = k[:, :NOPE].astype(jnp.bfloat16)
        turned = pltpu.roll(k[:, NOPE:], ROPE, axis=1)
        kaug[1, :, :NOPE] = jnp.where(low, 0.0, turned).astype(jnp.bfloat16)
        kaug[1, :, NOPE:] = jnp.where(low, turned, rope_odd[...]).astype(jnp.bfloat16)
        v = jnp.dot(tokens, weights(s, 2, xi), preferred_element_type=jnp.float32)
        vbuf[...] = v.astype(jnp.bfloat16)

    def attend(k, parity):
        s, xi = where(k)
        kaug, vbuf = held[parity]
        for t in range(2):
            span = (3 + t) * tok
            hide = bias[t * tok:(t + 1) * tok, :span]
            for h in range(2):
                begin = pl.multiple_of(s * 2 * QK + h * NOPE, 128)
                q = qbuf[t, xi, :, pl.ds(begin, 2 * NOPE)]
                sc = lax.dot_general(
                    q, kaug[h, :span, :], (((1,), (1,)), ((), ())),
                    preferred_element_type=jnp.float32,
                )
                sc = sc * scale + hide
                peak = jnp.max(sc, axis=1, keepdims=True)
                expo = jnp.exp2(sc - peak)
                total = jnp.sum(expo, axis=1, keepdims=True)
                cols = slice(h * VDIM, (h + 1) * VDIM)
                mixed = jnp.dot(
                    expo.astype(jnp.bfloat16), vbuf[:span, cols],
                    preferred_element_type=jnp.float32,
                )
                obuf[t, s, xi, :, cols] = (mixed / total).astype(jnp.bfloat16)

    def give(k):
        s, xi = where(k)
        at = pl.multiple_of((2 * xi + core) * cw + s * 2 * VDIM, 128)
        landed = out.at[:, pl.ds(at, 2 * VDIM)]
        pltpu.make_async_copy(obuf.at[core, s, xi], landed, o_sem.at[0]).start()
        remote(obuf.at[1 - core, s, xi], landed, o_sem.at[1], o_sem.at[2], (seq, mate)).start()

    def act(kind, name):
        if kind == "send":
            send(name)
        else:
            take(name)

    steps = stages * nx
    between, current = {}, "setup"
    for kind, name in [("piece", "setup")] + order:
        if kind != "piece":
            between[current].append((kind, name))
        elif name == "setup":
            current = "setup" if not between else "ready"
            between[current] = []
        else:
            current = name
            between[current] = []

    def events(name):
        for kind, what in between[name]:
            act(kind, what)

    def events_of(j, low, high, back):
        if not any(between["both", 2 * k + 1 + back] for k in range(low, high)):
            return
        if high - low == 1:
            events(("both", 2 * low + 1 + back))
            return
        middle = (low + high) // 2
        pl.when(j < middle)(functools.partial(events_of, j, low, middle, back))
        pl.when(j >= middle)(functools.partial(events_of, j, middle, high, back))

    events("setup")
    for xi in range(nx):
        q_copy(xi).start()
    setup()
    events("ready")
    project(0, 0)
    events(("first", 0))

    def pair(j, carry):
        for back in range(2):
            k = 2 * j + back
            project(k + 1, 1 - back)
            attend(k, back)
            give(k)
            events_of(j, 0, steps // 2 - 1, back)
        return carry

    lax.fori_loop(0, steps // 2 - 1, pair, 0)
    attend(steps - 2, 0)
    give(steps - 2)
    events(("last", steps - 2))
    project(steps - 1, 1)
    events(("first", steps - 1))
    attend(steps - 1, 1)
    give(steps - 1)
    events(("last", steps - 1))

    for i, kind in enumerate(SEND_KINDS):
        await_bytes(tiles(sent_tiles[kind]), w_send.at[i])
    await_bytes(tiles(3 * tok * (rank + ROPE) * 2 // 4096), lat_send.at[0])
    await_bytes(qbuf.at[core], q_send.at[0])
    await_bytes(obuf.at[core], o_sem.at[0])
    await_bytes(obuf.at[1 - core], o_sem.at[1])
    await_bytes(obuf.at[core], o_sem.at[2])


def shards(queries, latent, rope_keys, key_weight, value_weight, doc_lengths):
    n_seq, n_head = lax.axis_size("seq"), lax.axis_size("head")
    nx = n_head // 2
    tok, rank = latent.shape
    stages = key_weight.shape[1] // (2 * NOPE)
    docs = doc_lengths.shape[0]
    count = len({m.group for m in weight_messages(nx, n_seq // NY)})
    anywhere = pl.BlockSpec(memory_space=pl.ANY)
    dma = pltpu.SemaphoreType.DMA
    bf16 = jnp.bfloat16
    return pl.pallas_call(
        functools.partial(kernel, (n_seq, n_head, stages)),
        out_shape=jax.ShapeDtypeStruct((tok, n_head * stages * 2 * VDIM), bf16),
        in_specs=[anywhere] * 6,
        out_specs=anywhere,
        scratch_shapes=[
            pltpu.VMEM((UNITS * stages, nx, n_seq // NY, NY, key_weight.shape[0], 128), bf16),
            pltpu.VMEM((4, tok, rank), bf16),
            pltpu.VMEM((4, ROPE, tok), bf16),
            pltpu.VMEM((2, nx, tok, 2 * stages * QK), bf16),
            pltpu.VMEM((2, 4 * tok, 2 * NOPE), bf16),
            pltpu.VMEM((2, 4 * tok, 2 * NOPE), bf16),
            pltpu.VMEM((4 * tok, 2 * ROPE), jnp.float32),
            pltpu.VMEM((4 * tok, 2 * VDIM), bf16),
            pltpu.VMEM((4 * tok, 2 * VDIM), bf16),
            pltpu.VMEM((2 * tok, 4 * tok), jnp.float32),
            pltpu.VMEM((2, stages, nx, tok, 2 * VDIM), bf16),
            pltpu.VMEM((1, docs), jnp.int32),
            dma((1,)),
            dma((4,)),
            dma((4,)),
            dma((1,)),
            dma((1,)),
            dma((count,)),
            dma((len(SEND_KINDS),)),
            dma((2,)),
            dma((1,)),
            dma((3,)),
        ],
        compiler_params=pltpu.CompilerParams(collective_id=0, has_side_effects=True),
    )(queries, latent, rope_keys.T, key_weight, value_weight, doc_lengths.reshape(1, docs))


def solution(mesh):
    placed = (
        P(("seq", "head"), None),
        P(("seq", "head"), None),
        P(("seq", "head"), None),
        P("seq", "head"),
        P("seq", "head"),
        P(),
    )
    return jax.shard_map(
        shards, mesh=mesh, in_specs=placed, out_specs=P(("seq", "head"), None), check_vma=False
    )
```

time: 91.2 us -> 75.2 us (0.82)
  Pallas kernels: 85.4 us -> 72 us
  other arithmetic: 1.61 us -> 0 us
    pallas_call x1, Pallas kernels: 85.4 us -> 72 us  [shards(): pl.pallas_call(functools.partial(kernel, (n_seq, n_head, stages)), out_sh...]
    concatenate x1 -> x0, other arithmetic: 1.61 us -> none  [shards(): jnp.concatenate([latent, rope_keys, jnp.zeros((tok, 2 * ROPE - rope_keys....]
    unnamed x2 -> x1, local copies, waits for them, and re-layouts: 3.92 us -> 3.1 us
where the time goes in v2:
time: 75.2 us; the launch traced here: 75.1 us
  Pallas kernels  72 us (96%)
  local copies, waits for them, and re-layouts  3.1 us (4%)
    pallas_call x1, Pallas kernels, shards(): pl.pallas_call(functools.partial(kernel, (n_seq, n_head, stages)), out_sh...  72 us
    unnamed x1, local copies, waits for them, and re-layouts  3.1 us

profile of v2, /device:TPU:1, one launch (start us, length us, event | category | flops | bytes accessed | tf_op | source)
XLA Modules:
  0.0 75.1 jit_solution(15031157214011318364)
XLA Ops:
  0.0 72.0 %shard_map.64 = bf16[128,8192]{1,0:T(8,128)(2,1)} custom-call(bf16[128,12288]{1,0:T(8,128)(2,1)} %queries.1, bf16[128,512]{1,0:T(8,128)(2,1)} %latent.1, bf16[64,128]{1,0:T(8,128)(2,1)} %bitcast.2, bf16[16,1024]{1,0:T(8,128)(2,1)} %key_weight.1, bf16[16,1024]{1,0:T(8,128)(2,1)} %value_weight.1, s32[1,128]{1,0:T(1,128)} %bitcast.3), custom_call_target="tpu_custom_call" | custom-call | tf_op jit(solution)/shard_map/pallas_call | solution.py:458
  72.0 3.1 %copy.8 = bf16[128,8192]{1,0:T(8,128)(2,1)} copy(bf16[128,8192]{1,0:T(8,128)(2,1)} %shard_map.64) | data formatting | bytes 4194304

commit v3 on v2

--- a/solution.py
+++ b/solution.py
@@ -26,8 +26,10 @@
 BACKLOG = 0.7
 SEND_COST = 0.04
 WAIT_COST = 0.02
-LENGTH = {"first": 0.4, "both": 0.9, "last": 0.6, "setup": 0.8}
+LENGTH = {"block": 0.8, "setup": 0.8}
+DEPTH = 3
 OFFSETS = (0, -1, 1, 2)
+CHUNK = 32
 
 
 class Message:
@@ -114,13 +116,9 @@
 def make_plan(messages):
     pieces = [("setup", {("next",), ("mate",), ("share",)})]
     steps = [(s, off) for s in range(len(STAGES)) for off in OFFSETS]
-    for k, (s, off) in enumerate(steps):
-        kind = "first" if k == 0 else "both"
-        if k == len(steps) - 1:
-            pieces.append((("last", k - 1), set()))
-            kind = "first"
-        pieces.append(((kind, k), step_needs(messages, s, off)))
-    pieces.append((("last", len(steps) - 1), set()))
+    for b in range(len(steps) + DEPTH):
+        needed = step_needs(messages, *steps[b]) if b < len(steps) else set()
+        pieces.append((("block", b), needed))
     group_of = {m.name: m.group for m in messages}
     left = {}
     for m in messages:
@@ -166,7 +164,8 @@
 
 def kernel(
     sizes, queries, latent, rope, key_weight, value_weight, lengths, out,
-    w, lat, rope_all, qbuf, kaug0, kaug1, rope_odd, vbuf0, vbuf1, bias, obuf, len_buf,
+    w, lat, rope_all, qbuf, kaug0, kaug1, rope_odd, vbuf0, vbuf1, sbuf0, sbuf1, pbuf0, pbuf1,
+    inv0, inv1, bias, obuf, len_buf,
     own_sem, lat_sem, rope_sem, len_sem, lat_send, w_recv, w_send, q_sem, q_send, o_sem,
 ):
     n_seq, n_head, stages = sizes
@@ -316,11 +315,13 @@
             for kaug in (kaug0, kaug1):
                 kaug[0, rows, NOPE:] = tail.astype(jnp.bfloat16)
             rope_odd[rows, :] = pltpu.roll(tail, ROPE, axis=1)
+        for pbuf in (pbuf0, pbuf1):
+            pbuf[:, :tok, 3 * tok:] = jnp.zeros((2, tok, tok), jnp.bfloat16)
         for t in range(2):
             await_bytes(qbuf.at[t], q_sem.at[t])
 
     scale = LOG2E / math.sqrt(QK)
-    held = ((kaug0, vbuf0), (kaug1, vbuf1))
+    held = ((kaug0, vbuf0, sbuf0, pbuf0, inv0), (kaug1, vbuf1, sbuf1, pbuf1, inv1))
 
     def where(k):
         s, turn = k // nx, k % nx
@@ -333,42 +334,56 @@
         parts = [w[UNITS * s + j + i, xi].reshape(n_seq * 16, 128) for i in range(2)]
         return jnp.concatenate(parts, axis=1)
 
-    def project(k, parity):
+    def project_keys(k, parity):
         s, xi = where(k)
-        kaug, vbuf = held[parity]
-        tokens = lat[...].reshape(keys, rank)
+        kaug = held[parity][0]
         low = lax.broadcasted_iota(jnp.int32, (keys, NOPE), 1) < ROPE
-        k = jnp.dot(tokens, weights(s, 0, xi), preferred_element_type=jnp.float32)
+        k = jnp.dot(lat[...].reshape(keys, rank), weights(s, 0, xi), preferred_element_type=jnp.float32)
         kaug[0, :, :NOPE] = k[:, :NOPE].astype(jnp.bfloat16)
         turned = pltpu.roll(k[:, NOPE:], ROPE, axis=1)
         kaug[1, :, :NOPE] = jnp.where(low, 0.0, turned).astype(jnp.bfloat16)
         kaug[1, :, NOPE:] = jnp.where(low, turned, rope_odd[...]).astype(jnp.bfloat16)
-        v = jnp.dot(tokens, weights(s, 2, xi), preferred_element_type=jnp.float32)
-        vbuf[...] = v.astype(jnp.bfloat16)
-
-    def attend(k, parity):
+
+    def project_values(k, parity):
         s, xi = where(k)
-        kaug, vbuf = held[parity]
+        v = jnp.dot(lat[...].reshape(keys, rank), weights(s, 2, xi), preferred_element_type=jnp.float32)
+        held[parity][1][...] = v.astype(jnp.bfloat16)
+
+    def score(k, parity):
+        s, xi = where(k)
+        kaug, _, sbuf, _, _ = held[parity]
+        for h in range(2):
+            begin = pl.multiple_of(s * 2 * QK + h * NOPE, 128)
+            q = qbuf[:, xi, :, pl.ds(begin, 2 * NOPE)].reshape(2 * tok, 2 * NOPE)
+            sc = lax.dot_general(
+                q, kaug[h], (((1,), (1,)), ((), ())), preferred_element_type=jnp.float32
+            )
+            for t in range(2):
+                rows, span = slice(t * tok, (t + 1) * tok), (3 + t) * tok
+                sbuf[h, rows, :span] = sc[rows, :span] * scale + bias[rows, :span]
+
+    def soften(parity):
+        _, _, sbuf, pbuf, inv = held[parity]
         for t in range(2):
             span = (3 + t) * tok
-            hide = bias[t * tok:(t + 1) * tok, :span]
             for h in range(2):
-                begin = pl.multiple_of(s * 2 * QK + h * NOPE, 128)
-                q = qbuf[t, xi, :, pl.ds(begin, 2 * NOPE)]
-                sc = lax.dot_general(
-                    q, kaug[h, :span, :], (((1,), (1,)), ((), ())),
-                    preferred_element_type=jnp.float32,
-                )
-                sc = sc * scale + hide
-                peak = jnp.max(sc, axis=1, keepdims=True)
-                expo = jnp.exp2(sc - peak)
-                total = jnp.sum(expo, axis=1, keepdims=True)
-                cols = slice(h * VDIM, (h + 1) * VDIM)
-                mixed = jnp.dot(
-                    expo.astype(jnp.bfloat16), vbuf[:span, cols],
-                    preferred_element_type=jnp.float32,
-                )
-                obuf[t, s, xi, :, cols] = (mixed / total).astype(jnp.bfloat16)
+                for r in range(0, tok, CHUNK):
+                    rows = slice(t * tok + r, t * tok + r + CHUNK)
+                    sc = sbuf[h, rows, :span]
+                    expo = jnp.exp2(sc - jnp.max(sc, axis=1, keepdims=True))
+                    total = jnp.sum(expo, axis=1, keepdims=True)
+                    inv[h, rows, :] = jnp.broadcast_to(1.0 / total, (CHUNK, VDIM))
+                    pbuf[h, rows, :span] = expo.astype(jnp.bfloat16)
+
+    def mix(k, parity):
+        s, xi = where(k)
+        _, vbuf, _, pbuf, inv = held[parity]
+        for h in range(2):
+            cols = slice(h * VDIM, (h + 1) * VDIM)
+            mixed = jnp.dot(pbuf[h], vbuf[:, cols], preferred_element_type=jnp.float32)
+            mixed = (mixed * inv[h]).astype(jnp.bfloat16)
+            for t in range(2):
+                obuf[t, s, xi, :, cols] = mixed[t * tok:(t + 1) * tok]
 
     def give(k):
         s, xi = where(k)
@@ -400,41 +415,48 @@
             act(kind, what)
 
     def events_of(j, low, high, back):
-        if not any(between["both", 2 * k + 1 + back] for k in range(low, high)):
+        if not any(between["block", DEPTH + 2 * k + back] for k in range(low, high)):
             return
         if high - low == 1:
-            events(("both", 2 * low + 1 + back))
+            events(("block", DEPTH + 2 * low + back))
             return
         middle = (low + high) // 2
         pl.when(j < middle)(functools.partial(events_of, j, low, middle, back))
         pl.when(j >= middle)(functools.partial(events_of, j, middle, high, back))
+
+    def run(b, turn, first, last):
+        if first <= 1 <= last:
+            score(b - 1, (turn - 1) % 2)
+        if first <= 2 <= last:
+            soften(turn % 2)
+        if first <= 0 <= last:
+            project_keys(b, turn % 2)
+        if first <= 2 <= last:
+            project_values(b - 2, turn % 2)
+        if first <= 3 <= last:
+            mix(b - 3, (turn - 3) % 2)
+            give(b - 3)
 
     events("setup")
     for xi in range(nx):
         q_copy(xi).start()
     setup()
     events("ready")
-    project(0, 0)
-    events(("first", 0))
+    for b in range(DEPTH):
+        run(b, b, 0, b)
+        events(("block", b))
+    pairs = (steps - DEPTH) // 2
 
     def pair(j, carry):
         for back in range(2):
-            k = 2 * j + back
-            project(k + 1, 1 - back)
-            attend(k, back)
-            give(k)
-            events_of(j, 0, steps // 2 - 1, back)
+            run(DEPTH + 2 * j + back, DEPTH + back, 0, DEPTH)
+            events_of(j, 0, pairs, back)
         return carry
 
-    lax.fori_loop(0, steps // 2 - 1, pair, 0)
-    attend(steps - 2, 0)
-    give(steps - 2)
-    events(("last", steps - 2))
-    project(steps - 1, 1)
-    events(("first", steps - 1))
-    attend(steps - 1, 1)
-    give(steps - 1)
-    events(("last", steps - 1))
+    lax.fori_loop(0, pairs, pair, 0)
+    for b in range(DEPTH + 2 * pairs, steps + DEPTH):
+        run(b, b, max(0, b - steps + 1), DEPTH)
+        events(("block", b))
 
     for i, kind in enumerate(SEND_KINDS):
         await_bytes(tiles(sent_tiles[kind]), w_send.at[i])
@@ -470,6 +492,12 @@
             pltpu.VMEM((4 * tok, 2 * ROPE), jnp.float32),
             pltpu.VMEM((4 * tok, 2 * VDIM), bf16),
             pltpu.VMEM((4 * tok, 2 * VDIM), bf16),
+            pltpu.VMEM((2, 2 * tok, 4 * tok), jnp.float32),
+            pltpu.VMEM((2, 2 * tok, 4 * tok), jnp.float32),
+            pltpu.VMEM((2, 2 * tok, 4 * tok), bf16),
+            pltpu.VMEM((2, 2 * tok, 4 * tok), bf16),
+            pltpu.VMEM((2, 2 * tok, VDIM), jnp.float32),
+            pltpu.VMEM((2, 2 * tok, VDIM), jnp.float32),
             pltpu.VMEM((2 * tok, 4 * tok), jnp.float32),
             pltpu.VMEM((2, stages, nx, tok, 2 * VDIM), bf16),
             pltpu.VMEM((1, docs), jnp.int32),

time: 75.2 us -> 63.3 us (0.84)
  Pallas kernels: 72 us -> 60.1 us
    pallas_call x1, Pallas kernels: 72 us -> 60.1 us  [shards(): pl.pallas_call(functools.partial(kernel, (n_seq, n_head, stages)), out_sh...]
where the time goes in v3:
time: 63.3 us; the launch traced here: 63.2 us
  Pallas kernels  60.1 us (95%)
  local copies, waits for them, and re-layouts  3.1 us (5%)
    pallas_call x1, Pallas kernels, shards(): pl.pallas_call(functools.partial(kernel, (n_seq, n_head, stages)), out_sh...  60.1 us
    unnamed x1, local copies, waits for them, and re-layouts  3.1 us

profile of v3, /device:TPU:1, one launch (start us, length us, event | category | flops | bytes accessed | tf_op | source)
XLA Modules:
  0.0 63.2 jit_solution(6096191474474445995)
XLA Ops:
  0.0 60.1 %shard_map.64 = bf16[128,8192]{1,0:T(8,128)(2,1)} custom-call(bf16[128,12288]{1,0:T(8,128)(2,1)} %queries.1, bf16[128,512]{1,0:T(8,128)(2,1)} %latent.1, bf16[64,128]{1,0:T(8,128)(2,1)} %bitcast.2, bf16[16,1024]{1,0:T(8,128)(2,1)} %key_weight.1, bf16[16,1024]{1,0:T(8,128)(2,1)} %value_weight.1, s32[1,128]{1,0:T(1,128)} %bitcast.3), custom_call_target="tpu_custom_call" | custom-call | tf_op jit(solution)/shard_map/pallas_call | solution.py:480
  60.1 3.1 %copy.8 = bf16[128,8192]{1,0:T(8,128)(2,1)} copy(bf16[128,8192]{1,0:T(8,128)(2,1)} %shard_map.64) | data formatting | bytes 4194304
